TPU v7x, 32 devices: a whole 2x2x4 slice. The times are simulated.
32 devices in a mesh: gz: 8 (over y, x, core), xy: 4 (over z).
Axes of the slice: x: 2, y: 2, z: 4, core: 2. Of those that a mesh axis runs over, the one named last changes fastest.
Arguments:
- patches: bfloat16 [8, 8, 16, 128, 128], P('gz', 'xy'), may hold values from -6 to 6
- peak_offsets: int32 [8, 6, 8, 16], P('gz', None, 'xy'), may hold values from -4 to 4
- valid_masks: int32 [8, 3, 8, 16], P('gz', None, 'xy'), may hold values 0 or 1
- initial_positions: float32 [2, 8, 128, 256], P(None, 'gz', 'xy'), may hold values from -40 to 40
Outputs:
- positions: float32 [2, 8, 128, 256], P(None, 'gz', 'xy')
- targets: float32 [8, 6, 8, 16], P('gz', None, 'xy')
- surfaces: bfloat16 [8, 3, 8, 16, 128, 128], P('gz', None, 'xy')
- force_rms: float32 [4], replicated
All inputs are finite; a program needn't handle non-finite values. No bound on the sum of `valid_masks` on one device may be relied on, other than what follows from the above.
Results may differ from a plain program's by a relative error of at most 0.0091.
Values may be sent and summed in bfloat16 or wider, within the bound.
A program may use at most 64 MiB of HBM per device.

v0:
```python
import math

import jax
import jax.numpy as jnp
from jax import lax
from jax.sharding import PartitionSpec as P

SUB = 16
ITERS = 4


lattice_stiff = 0.5
clip_level = 5.0
step_size = 0.2
floor_ratio = 0.4
tiny_eps = 1e-06


def from_behind(array, axis, by):
    count = lax.axis_size(axis)
    pairs = [(i, i + by) for i in range(count) if 0 <= i + by < count]
    return lax.ppermute(array, axis, pairs)


def extended(block, sides, width):
    for axis, dim in sides:
        count = lax.axis_size(axis)
        forward = [(i, i + 1) for i in range(count - 1)]
        backward = [(target, source) for source, target in forward]
        low = lax.ppermute(
            lax.slice_in_dim(block, block.shape[dim] - width, None, axis=dim), axis, forward
        )
        high = lax.ppermute(lax.slice_in_dim(block, 0, width, axis=dim), axis, backward)
        block = jnp.concatenate([low, block, high], axis=dim)
    return block


def dft_tables(length):
    series = jnp.arange(length, dtype=jnp.int32)
    product = series[:, None] * series[None, :] % length
    angles = 2.0 * math.pi / length * product.astype(jnp.float32)
    return (jnp.cos(angles).astype(jnp.bfloat16), jnp.sin(angles).astype(jnp.bfloat16))


def right_product(left, table):
    return jnp.einsum("pab,bk->pak", left, table, preferred_element_type=jnp.float32)


def left_product(table, right):
    return jnp.einsum("ja,pak->pjk", table, right, preferred_element_type=jnp.float32)


def spectrum(tiles, cosine, sine):
    row_cos = right_product(tiles, cosine).astype(jnp.bfloat16)
    row_sin = right_product(tiles, sine).astype(jnp.bfloat16)
    real = left_product(cosine, row_cos) - left_product(sine, row_sin)
    imag = -(left_product(sine, row_cos) + left_product(cosine, row_sin))
    return (real, imag)


def correlate(first, second, cosine, sine, length):
    cross_real = (first[0] * second[0] + first[1] * second[1]).astype(jnp.bfloat16)
    cross_imag = (first[0] * second[1] - first[1] * second[0]).astype(jnp.bfloat16)
    half_real = (right_product(cross_real, cosine) - right_product(cross_imag, sine)).astype(
        jnp.bfloat16
    )
    half_imag = (right_product(cross_real, sine) + right_product(cross_imag, cosine)).astype(
        jnp.bfloat16
    )
    whole = left_product(cosine, half_real) - left_product(sine, half_imag)
    return whole / float(length * length)


def refine(corr, shift_rows, shift_cols, length):
    series = jnp.arange(length, dtype=jnp.int32)
    taps = jnp.arange(3, dtype=jnp.int32) - 1
    row_index = (shift_rows[:, None] + taps[None, :] + length) % length
    col_index = (shift_cols[:, None] + taps[None, :] + length) % length
    row_pick = (series[None, None, :] == row_index[:, :, None]).astype(jnp.float32)
    col_pick = (series[None, None, :] == col_index[:, :, None]).astype(jnp.float32)
    partial_rows = jnp.einsum("pta,pab->ptb", row_pick, corr, precision=lax.Precision.HIGHEST)
    values = jnp.einsum("ptb,psb->pts", partial_rows, col_pick, precision=lax.Precision.HIGHEST)
    floor_value = floor_ratio * length
    along_rows = values[:, :, 1]
    along_cols = values[:, 1, :]
    sub_rows = (along_rows[:, 2] - along_rows[:, 0]) / jnp.maximum(
        jnp.sum(jnp.abs(along_rows), axis=1), floor_value
    )
    sub_cols = (along_cols[:, 2] - along_cols[:, 0]) / jnp.maximum(
        jnp.sum(jnp.abs(along_cols), axis=1), floor_value
    )
    return (shift_rows.astype(jnp.float32) + sub_rows, shift_cols.astype(jnp.float32) + sub_cols)


def expand_nodes(array, axis):
    return jnp.repeat(jnp.repeat(array, SUB, axis=axis), SUB, axis=axis + 1)


def local(patches, peak_offsets, valid_masks, initial_positions):
    length = patches.shape[-1]
    rows_dev = patches.shape[1]
    columns = patches.shape[2]
    tiles_count = rows_dev * columns
    cosine, sine = dft_tables(length)
    own = spectrum(patches.reshape(tiles_count, length, length), cosine, sine)
    offsets = peak_offsets.reshape(6, tiles_count)
    results = []
    maps = []
    for distance in range(1, 4):
        other_tiles = from_behind(patches, "gz", -distance)
        other = spectrum(other_tiles.reshape(tiles_count, length, length), cosine, sine)
        corr = correlate(own, other, cosine, sine, length)
        maps.append(corr.astype(jnp.bfloat16).reshape(rows_dev, columns, length, length))
        rows_target, cols_target = refine(
            corr, offsets[2 * distance - 2], offsets[2 * distance - 1], length
        )
        results.append(rows_target)
        results.append(cols_target)
    targets = jnp.stack(results).reshape(1, 6, rows_dev, columns)
    surfaces = jnp.stack(maps).reshape(1, 3, rows_dev, columns, length, length)
    depth_count = lax.axis_size("gz")
    depth_index = lax.axis_index("gz")
    tile_index = lax.axis_index("xy")
    tile_count = lax.axis_size("xy")
    weights = []
    vectors = []
    lower_weights = []
    lower_vectors = []
    for distance in range(1, 4):
        live = (depth_index + distance < depth_count).astype(jnp.float32)
        weight = valid_masks[:, distance - 1].astype(jnp.float32) * (1.0 / distance) * live
        vector = jnp.stack([targets[:, 2 * distance - 2], targets[:, 2 * distance - 1]], axis=0)
        vector_low, weight_low = from_behind((vector, weight), "gz", distance)
        weights.append(expand_nodes(weight, 1))
        vectors.append(expand_nodes(vector, 2))
        lower_weights.append(expand_nodes(weight_low, 1))
        lower_vectors.append(expand_nodes(vector_low, 2))
    count = 2.0 * depth_count * tile_count * initial_positions.shape[2] * initial_positions.shape[3]
    positions = initial_positions
    norms = []
    for iteration in range(ITERS):
        padded = extended(positions.astype(jnp.bfloat16), (("xy", 2),), 1).astype(positions.dtype)
        top_row = jnp.where(tile_index == 0, positions[:, :, :1], padded[:, :, :1])
        bottom_row = jnp.where(
            tile_index == tile_count - 1, positions[:, :, -1:], padded[:, :, -1:]
        )
        upper_rows = jnp.concatenate([top_row, positions[:, :, :-1]], axis=2)
        lower_rows = jnp.concatenate([positions[:, :, 1:], bottom_row], axis=2)
        edged = jnp.pad(positions, ((0, 0), (0, 0), (0, 0), (1, 1)), mode="edge")
        lattice = (
            upper_rows + lower_rows + edged[:, :, :, :-2] + edged[:, :, :, 2:] - 4.0 * positions
        )
        force = lattice_stiff * lattice
        climbing = positions
        sinking = positions
        for distance in range(1, 4):
            climbing = from_behind(climbing.astype(jnp.bfloat16), "gz", -1).astype(climbing.dtype)
            sinking = from_behind(sinking.astype(jnp.bfloat16), "gz", 1).astype(sinking.dtype)
            force = force + weights[distance - 1] * (climbing - positions - vectors[distance - 1])
            force = force - lower_weights[distance - 1] * (
                positions - sinking - lower_vectors[distance - 1]
            )
        total = lax.psum(jnp.sum(force * force), ("gz", "xy"))
        rms = jnp.sqrt(total / count + tiny_eps)
        factor = jnp.minimum(1.0, clip_level / rms)
        positions = positions + step_size * factor * force
        norms.append(rms)
    return (positions, targets, surfaces, jnp.stack(norms))


def solution(mesh):
    in_specs = (
        P("gz", "xy", None, None, None),
        P("gz", None, "xy", None),
        P("gz", None, "xy", None),
        P(None, "gz", "xy", None),
    )
    out_specs = (
        P(None, "gz", "xy", None),
        P("gz", None, "xy", None),
        P("gz", None, "xy", None, None, None),
        P(),
    )
    return jax.shard_map(local, mesh=mesh, in_specs=in_specs, out_specs=out_specs, check_vma=False)
```

profile of v0, /device:TPU:0, one launch (start us, length us, event | category | flops | bytes accessed | tf_op | source)
XLA Modules:
  0.0 432.7 jit_solution(15893436551344031341)
XLA Ops:
  6.1 3.6 collective-permute-start.5
  10.5 4.5 %collective-permute-start.4 = (f32[1,2,16]{2,1,0:T(2,128)S(1)}, f32[1,2,16]{2,1,0:T(2,128)S(1)}, u32[]{:S(2)}, u32[]{:S(2)}) collective-permute-start(f32[1,2,16]{2,1,0:T(2,128)S(1)} %get-tuple-element.93), channel_id=1, source_target_pairs={{0,4},{4,8},{8,12},{12,16},{16,20},{20,24},{24,28},{1,5},{5,9},{9,... | collective-permute-start | bytes 392 | tf_op jit(solution)/shard_map/ppermute | solution.py:22
  25.0 4.9 %collective-permute-start.9 = (f32[1,2,16]{2,1,0:T(2,128)S(1)}, f32[1,2,16]{2,1,0:T(2,128)S(1)}, u32[]{:S(2)}, u32[]{:S(2)}) collective-permute-start(f32[1,2,16]{2,1,0:T(2,128)S(1)} %get-tuple-element.92), channel_id=1, source_target_pairs={{0,8},{4,12},{8,16},{12,20},{16,24},{20,28},{1,9},{5,13},{9,17},{1... | collective-permute-start | bytes 392 | tf_op jit(solution)/shard_map/ppermute | solution.py:22
  31.2 16.6 %collective-permute-start.14 = (f32[1,2,16]{2,1,0:T(2,128)S(1)}, f32[1,2,16]{2,1,0:T(2,128)S(1)}, u32[]{:S(2)}, u32[]{:S(2)}) collective-permute-start(f32[1,2,16]{2,1,0:T(2,128)S(1)} %get-tuple-element.91), channel_id=1, source_target_pairs={{0,12},{4,16},{8,20},{12,24},{16,28},{1,13},{5,17},{9,21},{13,25},... | collective-permute-start | bytes 392 | tf_op jit(solution)/shard_map/ppermute | solution.py:22
  62.2 5.1 %collective-permute-start.10 = (bf16[2,1,32,256]{3,2,1,0:T(8,128)(2,1)}, bf16[2,1,32,256]{3,2,1,0:T(8,128)(2,1)}, u32[]{:S(2)}, u32[]{:S(2)}) collective-permute-start(bf16[2,1,32,256]{3,2,1,0:T(8,128)(2,1)} %collective-permute-done.5), channel_id=1, source_target_pairs={{0,4},{4,8},{8,12},{12,16},{16,20},{20,24},{24,28},{1,5},{5,9},{9,... | collective-permute-start | bytes 98312 | tf_op jit(solution)/shard_map/ppermute | solution.py:22
  69.2 13.2 %collective-permute-start.15 = (bf16[2,1,32,256]{3,2,1,0:T(8,128)(2,1)}, bf16[2,1,32,256]{3,2,1,0:T(8,128)(2,1)}, u32[]{:S(2)}, u32[]{:S(2)}) collective-permute-start(bf16[2,1,32,256]{3,2,1,0:T(8,128)(2,1)} %collective-permute-done.10), channel_id=1, source_target_pairs={{0,4},{4,8},{8,12},{12,16},{16,20},{20,24},{24,28},{1,5},{5,9},{9,... | collective-permute-start | bytes 98312 | tf_op jit(solution)/shard_map/ppermute | solution.py:22
  101.2 4.3 fusion.16
  109.5 4.1 fusion.8
  113.6 5.1 %fusion.352 = (bf16[32,128,128]{2,1,0:T(8,128)(2,1)}, f32[32,128,128]{2,1,0:T(8,128)}) fusion(f32[32,128,128]{2,1,0:T(8,128)} %fusion.8, f32[32,128,128]{2,1,0:T(8,128)} %fusion.96, bf16[32,128,128]{1,2,0:T(8,128)(2,1)S(1)} %copy-done.2), kind=kOutput, calls=%fused_computation.407 | convolution fusion | flops 271548416 | bytes 8388608 | tf_op jit(solution)/shard_map/ja,pak->pjk/dot_general | solution.py:50
  127.7 4.1 fusion.9
  131.8 5.1 %fusion.349 = (bf16[32,128,128]{2,1,0:T(8,128)(2,1)}, f32[32,128,128]{2,1,0:T(8,128)}) fusion(f32[32,128,128]{2,1,0:T(8,128)} %fusion.9, f32[32,128,128]{2,1,0:T(8,128)} %fusion.88, bf16[32,128,128]{1,2,0:T(8,128)(2,1)S(1)} %copy-done.1), kind=kOutput, calls=%fused_computation.406 | convolution fusion | flops 271548416 | bytes 8388608 | tf_op jit(solution)/shard_map/ja,pak->pjk/dot_general | solution.py:50
  146.0 4.5 %fusion.10 = f32[32,128,128]{2,1,0:T(8,128)} fusion(f32[32,128,128]{2,1,0:T(8,128)} %fusion.113, bf16[32,128,128]{1,2,0:T(8,128)(2,1)S(1)} %copy-done), kind=kOutput, calls=%fused_computation.42 | convolution fusion | flops 269975552 | bytes 5242880 | tf_op jit(solution)/shard_map/ja,pak->pjk/dot_general | solution.py:50
  150.5 4.4 %fusion.346 = (bf16[32,128,128]{2,1,0:T(8,128)(2,1)}, f32[32,128,128]{2,1,0:T(8,128)}) fusion(f32[32,128,128]{2,1,0:T(8,128)} %fusion.10, f32[32,128,128]{2,1,0:T(8,128)S(1)} %copy-done.5, bf16[32,128,128]{1,2,0:T(8,128)(2,1)S(1)} %copy-done), kind=kOutput, calls=%fused_computation.405 | convolution fusion | flops 271548416 | bytes 8388608 | tf_op jit(solution)/shard_map/ja,pak->pjk/dot_general | solution.py:50
  163.8 7.3 %collective-permute-start.11 = (f32[2,1,2,16]{3,2,1,0:T(2,128)}, f32[2,1,2,16]{3,2,1,0:T(2,128)}, u32[]{:S(2)}, u32[]{:S(2)}) collective-permute-start(f32[2,1,2,16]{3,2,1,0:T(2,128)} %get-tuple-element.99), channel_id=1, source_target_pairs={{0,8},{4,12},{8,16},{12,20},{16,24},{20,28},{1,9},{5,13},{9,17},{1... | collective-permute-start | bytes 776 | tf_op jit(solution)/shard_map/ppermute | solution.py:22
  187.6 40.1 %psum.28 = f32[]{:T(128)} all-reduce(f32[]{:T(128)} %get-tuple-element.40), channel_id=1, replica_groups=mesh['gz'=8,'xy'=4] {'gz','xy'}, use_global_device_ids=true, to_apply=%region_7.8 | all-reduce | flops 1 | bytes 8 | tf_op jit(solution)/shard_map/psum | solution.py:163
  237.3 4.2 collective-permute-start.22
  242.8 4.3 collective-permute-start.24
  248.7 45.8 %psum.29 = f32[]{:T(128)} all-reduce(f32[]{:T(128)} %get-tuple-element.36), channel_id=1, replica_groups=mesh['gz'=8,'xy'=4] {'gz','xy'}, use_global_device_ids=true, to_apply=%region_9.10 | all-reduce | flops 1 | bytes 8 | tf_op jit(solution)/shard_map/psum | solution.py:163
  305.6 4.2 collective-permute-start.30
  311.2 4.3 collective-permute-start.32
  317.0 45.8 %psum.30 = f32[]{:T(128)} all-reduce(f32[]{:T(128)} %get-tuple-element.32), channel_id=1, replica_groups=mesh['gz'=8,'xy'=4] {'gz','xy'}, use_global_device_ids=true, to_apply=%region_11.12 | all-reduce | flops 1 | bytes 8 | tf_op jit(solution)/shard_map/psum | solution.py:163
  372.9 4.2 collective-permute-start.38
  378.4 4.3 collective-permute-start.40
  384.3 46.0 %psum.31 = f32[]{:T(128)} all-reduce(f32[]{:T(128)} %get-tuple-element.28), channel_id=1, replica_groups=mesh['gz'=8,'xy'=4] {'gz','xy'}, use_global_device_ids=true, to_apply=%region_13.14 | all-reduce | flops 1 | bytes 8 | tf_op jit(solution)/shard_map/psum | solution.py:163
  (304 shorter events, 137.7 us)
Async XLA Ops:
  0.6 81.8 %collective-permute-start.13 = (bf16[1,2,16,128,128]{4,3,2,1,0:T(8,128)(2,1)}, bf16[1,2,16,128,128]{4,3,2,1,0:T(8,128)(2,1)}, u32[]{:S(2)}, u32[]{:S(2)}) collective-permute-start(bf16[1,2,16,128,128]{4,3,2,1,0:T(8,128)(2,1)} %param.4), channel_id=1, source_target_pairs={{12,0},{16,4},{20,8},{24,12},{28,16},{13,1},{17,5},{21,9},{25,13},... | collective-permute-start | bytes 3145736 | tf_op jit(solution)/shard_map/ppermute | solution.py:22
  2.1 84.3 %collective-permute-start.8 = (bf16[1,2,16,128,128]{4,3,2,1,0:T(8,128)(2,1)}, bf16[1,2,16,128,128]{4,3,2,1,0:T(8,128)(2,1)}, u32[]{:S(2)}, u32[]{:S(2)}) collective-permute-start(bf16[1,2,16,128,128]{4,3,2,1,0:T(8,128)(2,1)} %param.4), channel_id=1, source_target_pairs={{8,0},{12,4},{16,8},{20,12},{24,16},{28,20},{9,1},{13,5},{17,9},{2... | collective-permute-start | bytes 3145736 | tf_op jit(solution)/shard_map/ppermute | solution.py:22
  4.8 56.0 %collective-permute-start.2 = (bf16[2,1,32,256]{3,2,1,0:T(8,128)(2,1)}, bf16[2,1,32,256]{3,2,1,0:T(8,128)(2,1)}, u32[]{:S(2)}, u32[]{:S(2)}) collective-permute-start(bf16[2,1,32,256]{3,2,1,0:T(8,128)(2,1)} %convert_element_type.496), channel_id=1, source_target_pairs={{4,0},{8,4},{12,8},{16,12},{20,16},{24,20},{28,24},{5,1},{9,5},{13... | collective-permute-start | bytes 98312 | tf_op jit(solution)/shard_map/ppermute | solution.py:22
  6.1 56.1 %collective-permute-start.5 = (bf16[2,1,32,256]{3,2,1,0:T(8,128)(2,1)}, bf16[2,1,32,256]{3,2,1,0:T(8,128)(2,1)}, u32[]{:S(2)}, u32[]{:S(2)}) collective-permute-start(bf16[2,1,32,256]{3,2,1,0:T(8,128)(2,1)} %convert_element_type.496), channel_id=1, source_target_pairs={{0,4},{4,8},{8,12},{12,16},{16,20},{20,24},{24,28},{1,5},{5,9},{9,... | collective-permute-start | bytes 98312 | tf_op jit(solution)/shard_map/ppermute | solution.py:22
  10.5 14.6 %collective-permute-start.4 = (f32[1,2,16]{2,1,0:T(2,128)S(1)}, f32[1,2,16]{2,1,0:T(2,128)S(1)}, u32[]{:S(2)}, u32[]{:S(2)}) collective-permute-start(f32[1,2,16]{2,1,0:T(2,128)S(1)} %get-tuple-element.93), channel_id=1, source_target_pairs={{0,4},{4,8},{8,12},{12,16},{16,20},{20,24},{24,28},{1,5},{5,9},{9,... | collective-permute-start | bytes 392 | tf_op jit(solution)/shard_map/ppermute | solution.py:22
  31.2 17.9 %collective-permute-start.14 = (f32[1,2,16]{2,1,0:T(2,128)S(1)}, f32[1,2,16]{2,1,0:T(2,128)S(1)}, u32[]{:S(2)}, u32[]{:S(2)}) collective-permute-start(f32[1,2,16]{2,1,0:T(2,128)S(1)} %get-tuple-element.91), channel_id=1, source_target_pairs={{0,12},{4,16},{8,20},{12,24},{16,28},{1,13},{5,17},{9,21},{13,25},... | collective-permute-start | bytes 392 | tf_op jit(solution)/shard_map/ppermute | solution.py:22
  59.6 30.6 %collective-permute-start.3 = (bf16[1,2,16,128,128]{4,3,2,1,0:T(8,128)(2,1)S(1)}, bf16[1,2,16,128,128]{4,3,2,1,0:T(8,128)(2,1)S(1)}, u32[]{:S(2)}, u32[]{:S(2)}) collective-permute-start(bf16[1,2,16,128,128]{4,3,2,1,0:T(8,128)(2,1)S(1)} %copy-done.7), channel_id=1, source_target_pairs={{4,0},{8,4},{12,8},{16,12},{20,16},{24,20},{28,24},{5,1},{9,5},{13... | collective-permute-start | bytes 3145736 | tf_op jit(solution)/shard_map/ppermute | solution.py:22
  60.9 7.1 %collective-permute-start.7 = (bf16[2,1,32,256]{3,2,1,0:T(8,128)(2,1)}, bf16[2,1,32,256]{3,2,1,0:T(8,128)(2,1)}, u32[]{:S(2)}, u32[]{:S(2)}) collective-permute-start(bf16[2,1,32,256]{3,2,1,0:T(8,128)(2,1)} %collective-permute-done.2), channel_id=1, source_target_pairs={{4,0},{8,4},{12,8},{16,12},{20,16},{24,20},{28,24},{5,1},{9,5},{13... | collective-permute-start | bytes 98312 | tf_op jit(solution)/shard_map/ppermute | solution.py:22
  67.9 118.0 %collective-permute-start.12 = (bf16[2,1,32,256]{3,2,1,0:T(8,128)(2,1)}, bf16[2,1,32,256]{3,2,1,0:T(8,128)(2,1)}, u32[]{:S(2)}, u32[]{:S(2)}) collective-permute-start(bf16[2,1,32,256]{3,2,1,0:T(8,128)(2,1)} %collective-permute-done.7), channel_id=1, source_target_pairs={{4,0},{8,4},{12,8},{16,12},{20,16},{24,20},{28,24},{5,1},{9,5},{13... | collective-permute-start | bytes 98312 | tf_op jit(solution)/shard_map/ppermute | solution.py:22
  69.2 116.7 %collective-permute-start.15 = (bf16[2,1,32,256]{3,2,1,0:T(8,128)(2,1)}, bf16[2,1,32,256]{3,2,1,0:T(8,128)(2,1)}, u32[]{:S(2)}, u32[]{:S(2)}) collective-permute-start(bf16[2,1,32,256]{3,2,1,0:T(8,128)(2,1)} %collective-permute-done.10), channel_id=1, source_target_pairs={{0,4},{4,8},{8,12},{12,16},{16,20},{20,24},{24,28},{1,5},{5,9},{9,... | collective-permute-start | bytes 98312 | tf_op jit(solution)/shard_map/ppermute | solution.py:22
  159.5 24.5 %collective-permute-start.6 = (f32[2,1,2,16]{3,2,1,0:T(2,128)S(1)}, f32[2,1,2,16]{3,2,1,0:T(2,128)S(1)}, u32[]{:S(2)}, u32[]{:S(2)}) collective-permute-start(f32[2,1,2,16]{3,2,1,0:T(2,128)S(1)} %get-tuple-element.97), channel_id=1, source_target_pairs={{0,4},{4,8},{8,12},{12,16},{16,20},{20,24},{24,28},{1,5},{5,9},{9,... | collective-permute-start | bytes 776 | tf_op jit(solution)/shard_map/ppermute | solution.py:22
  163.8 20.6 %collective-permute-start.11 = (f32[2,1,2,16]{3,2,1,0:T(2,128)}, f32[2,1,2,16]{3,2,1,0:T(2,128)}, u32[]{:S(2)}, u32[]{:S(2)}) collective-permute-start(f32[2,1,2,16]{3,2,1,0:T(2,128)} %get-tuple-element.99), channel_id=1, source_target_pairs={{0,8},{4,12},{8,16},{12,20},{16,24},{20,28},{1,9},{5,13},{9,17},{1... | collective-permute-start | bytes 776 | tf_op jit(solution)/shard_map/ppermute | solution.py:22
  228.5 7.5 %collective-permute-start.19 = (bf16[2,1,32,256]{3,2,1,0:T(8,128)(2,1)S(1)}, bf16[2,1,32,256]{3,2,1,0:T(8,128)(2,1)S(1)}, u32[]{:S(2)}, u32[]{:S(2)}) collective-permute-start(bf16[2,1,32,256]{3,2,1,0:T(8,128)(2,1)S(1)} %get-tuple-element.38), channel_id=1, source_target_pairs={{4,0},{8,4},{12,8},{16,12},{20,16},{24,20},{28,24},{5,1},{9,5},{13... | collective-permute-start | bytes 98312 | tf_op jit(solution)/shard_map/ppermute | solution.py:22
  229.8 7.5 %collective-permute-start.20 = (bf16[2,1,32,256]{3,2,1,0:T(8,128)(2,1)S(1)}, bf16[2,1,32,256]{3,2,1,0:T(8,128)(2,1)S(1)}, u32[]{:S(2)}, u32[]{:S(2)}) collective-permute-start(bf16[2,1,32,256]{3,2,1,0:T(8,128)(2,1)S(1)} %get-tuple-element.38), channel_id=1, source_target_pairs={{0,4},{4,8},{8,12},{12,16},{16,20},{20,24},{24,28},{1,5},{5,9},{9,... | collective-permute-start | bytes 98312 | tf_op jit(solution)/shard_map/ppermute | solution.py:22
  232.8 14.3 %collective-permute-start.17 = (bf16[2,1,1,256]{3,2,1,0:T(2,128)(2,1)S(1)}, bf16[2,1,1,256]{3,2,1,0:T(2,128)(2,1)S(1)}, u32[]{:S(2)}, u32[]{:S(2)}) collective-permute-start(bf16[2,1,1,256]{3,2,1,0:T(2,128)(2,1)S(1)} %get-tuple-element.80), channel_id=1, source_target_pairs={{0,1},{1,2},{2,3},{4,5},{5,6},{6,7},{8,9},{9,10},{10,11},{12,13},{... | collective-permute-start | bytes 3080 | tf_op jit(solution)/shard_map/ppermute | solution.py:30
  234.6 12.5 %collective-permute-start.18 = (bf16[2,1,1,256]{3,2,1,0:T(2,128)(2,1)S(1)}, bf16[2,1,1,256]{3,2,1,0:T(2,128)(2,1)S(1)}, u32[]{:S(2)}, u32[]{:S(2)}) collective-permute-start(bf16[2,1,1,256]{3,2,1,0:T(2,128)(2,1)S(1)} %get-tuple-element.81), channel_id=1, source_target_pairs={{1,0},{2,1},{3,2},{5,4},{6,5},{7,6},{9,8},{10,9},{11,10},{13,12},{... | collective-permute-start | bytes 3080 | tf_op jit(solution)/shard_map/ppermute | solution.py:33
  295.2 9.1 %collective-permute-start.27 = (bf16[2,1,32,256]{3,2,1,0:T(8,128)(2,1)S(1)}, bf16[2,1,32,256]{3,2,1,0:T(8,128)(2,1)S(1)}, u32[]{:S(2)}, u32[]{:S(2)}) collective-permute-start(bf16[2,1,32,256]{3,2,1,0:T(8,128)(2,1)S(1)} %get-tuple-element.34), channel_id=1, source_target_pairs={{4,0},{8,4},{12,8},{16,12},{20,16},{24,20},{28,24},{5,1},{9,5},{13... | collective-permute-start | bytes 98312 | tf_op jit(solution)/shard_map/ppermute | solution.py:22
  296.5 9.1 %collective-permute-start.28 = (bf16[2,1,32,256]{3,2,1,0:T(8,128)(2,1)S(1)}, bf16[2,1,32,256]{3,2,1,0:T(8,128)(2,1)S(1)}, u32[]{:S(2)}, u32[]{:S(2)}) collective-permute-start(bf16[2,1,32,256]{3,2,1,0:T(8,128)(2,1)S(1)} %get-tuple-element.34), channel_id=1, source_target_pairs={{0,4},{4,8},{8,12},{12,16},{16,20},{20,24},{24,28},{1,5},{5,9},{9,... | collective-permute-start | bytes 98312 | tf_op jit(solution)/shard_map/ppermute | solution.py:22
  299.6 15.9 %collective-permute-start.25 = (bf16[2,1,1,256]{3,2,1,0:T(2,128)(2,1)S(1)}, bf16[2,1,1,256]{3,2,1,0:T(2,128)(2,1)S(1)}, u32[]{:S(2)}, u32[]{:S(2)}) collective-permute-start(bf16[2,1,1,256]{3,2,1,0:T(2,128)(2,1)S(1)} %get-tuple-element.78), channel_id=1, source_target_pairs={{0,1},{1,2},{2,3},{4,5},{5,6},{6,7},{8,9},{9,10},{10,11},{12,13},{... | collective-permute-start | bytes 3080 | tf_op jit(solution)/shard_map/ppermute | solution.py:30
  303.0 12.5 %collective-permute-start.26 = (bf16[2,1,1,256]{3,2,1,0:T(2,128)(2,1)S(1)}, bf16[2,1,1,256]{3,2,1,0:T(2,128)(2,1)S(1)}, u32[]{:S(2)}, u32[]{:S(2)}) collective-permute-start(bf16[2,1,1,256]{3,2,1,0:T(2,128)(2,1)S(1)} %get-tuple-element.79), channel_id=1, source_target_pairs={{1,0},{2,1},{3,2},{5,4},{6,5},{7,6},{9,8},{10,9},{11,10},{13,12},{... | collective-permute-start | bytes 3080 | tf_op jit(solution)/shard_map/ppermute | solution.py:33
  363.7 7.9 %collective-permute-start.35 = (bf16[2,1,32,256]{3,2,1,0:T(8,128)(2,1)S(1)}, bf16[2,1,32,256]{3,2,1,0:T(8,128)(2,1)S(1)}, u32[]{:S(2)}, u32[]{:S(2)}) collective-permute-start(bf16[2,1,32,256]{3,2,1,0:T(8,128)(2,1)S(1)} %get-tuple-element.30), channel_id=1, source_target_pairs={{4,0},{8,4},{12,8},{16,12},{20,16},{24,20},{28,24},{5,1},{9,5},{13... | collective-permute-start | bytes 98312 | tf_op jit(solution)/shard_map/ppermute | solution.py:22
  365.0 7.9 %collective-permute-start.36 = (bf16[2,1,32,256]{3,2,1,0:T(8,128)(2,1)S(1)}, bf16[2,1,32,256]{3,2,1,0:T(8,128)(2,1)S(1)}, u32[]{:S(2)}, u32[]{:S(2)}) collective-permute-start(bf16[2,1,32,256]{3,2,1,0:T(8,128)(2,1)S(1)} %get-tuple-element.30), channel_id=1, source_target_pairs={{0,4},{4,8},{8,12},{12,16},{16,20},{20,24},{24,28},{1,5},{5,9},{9,... | collective-permute-start | bytes 98312 | tf_op jit(solution)/shard_map/ppermute | solution.py:22
  368.0 14.7 %collective-permute-start.33 = (bf16[2,1,1,256]{3,2,1,0:T(2,128)(2,1)S(1)}, bf16[2,1,1,256]{3,2,1,0:T(2,128)(2,1)S(1)}, u32[]{:S(2)}, u32[]{:S(2)}) collective-permute-start(bf16[2,1,1,256]{3,2,1,0:T(2,128)(2,1)S(1)} %get-tuple-element.76), channel_id=1, source_target_pairs={{0,1},{1,2},{2,3},{4,5},{5,6},{6,7},{8,9},{9,10},{10,11},{12,13},{... | collective-permute-start | bytes 3080 | tf_op jit(solution)/shard_map/ppermute | solution.py:30
  370.3 12.5 %collective-permute-start.34 = (bf16[2,1,1,256]{3,2,1,0:T(2,128)(2,1)S(1)}, bf16[2,1,1,256]{3,2,1,0:T(2,128)(2,1)S(1)}, u32[]{:S(2)}, u32[]{:S(2)}) collective-permute-start(bf16[2,1,1,256]{3,2,1,0:T(2,128)(2,1)S(1)} %get-tuple-element.77), channel_id=1, source_target_pairs={{1,0},{2,1},{3,2},{5,4},{6,5},{7,6},{9,8},{10,9},{11,10},{13,12},{... | collective-permute-start | bytes 3080 | tf_op jit(solution)/shard_map/ppermute | solution.py:33
  (43 other events, 273.2 us)
where the time goes:
time: 439 us; the launch traced here: 433 us
  blocking collectives  178 us (41%)
  starting transfers between devices  130 us (30%)
  matrix products  79.1 us (18%)
  local copies, waits for them, and re-layouts  18.3 us (4%)
  other arithmetic  14 us (3%)
  waiting for transfers between devices  8.73 us (2%)
  between operations  5.25 us (1%)
    psum x4, blocking collectives, local(): total = lax.psum(jnp.sum(force * force), ('gz', 'xy'))  178 us
    ppermute x33, starting transfers between devices, from_behind(): return lax.ppermute(array, axis, pairs)  113 us
    dot_general x22, matrix products, left_product(): jnp.einsum('ja,pak->pjk', table, right, preferred_element_type=jnp.float32)  44.1 us
    dot_general x14, matrix products, right_product(): jnp.einsum('pab,bk->pak', left, table, preferred_element_type=jnp.float32)  23.8 us
    ppermute x4, starting transfers between devices, extended(): lax.ppermute(lax.slice_in_dim(block, block.shape[dim] - width, None, axis...  11 us
    dot_general x3, matrix products, refine(): jnp.einsum('pta,pab->ptb', row_pick, corr, precision=lax.Precision.HIGHEST)  10.2 us
  transfers between devices with their start and end apart: 41, of which 7 were waited for; matrix products, arithmetic and copies ran while one was open for 24% of the time, Pallas kernels for 0%

commit v1 on v0

v1 whole, which is shorter than its diff:
```python
import functools

import jax
import jax.numpy as jnp
import numpy as np
from jax import lax
from jax.experimental import pallas as pl
from jax.experimental.pallas import tpu as pltpu
from jax.sharding import PartitionSpec as P

SUB = 16
ITERS = 4
REACH = 3
GHOST = 8
GROUP = 4

lattice_stiff = 0.5
clip_level = 5.0
step_size = 0.2
floor_ratio = 0.4
tiny_eps = 1e-06

MESH = pl.DeviceIdType.MESH
F32 = jnp.float32
BF16 = jnp.bfloat16


def tables(length):
    series = np.arange(length, dtype=np.int64)
    product = (series[:, None] * series[None, :]) % length
    angles = np.float32(2.0 * np.pi / length) * product.astype(np.float32)
    cosine = np.cos(angles).astype(np.float32)
    sine = np.sin(angles).astype(np.float32)
    rows = np.concatenate([cosine, sine], axis=1)
    forward = np.block([[cosine, -sine], [-sine, -cosine]])
    back = np.block([[cosine, sine], [-sine, cosine]])
    last = np.concatenate([cosine, -sine], axis=1)
    return [jnp.asarray(t.astype(jnp.bfloat16)) for t in (rows, forward, back, last)]


def dot(left, right):
    return jnp.dot(left, right, preferred_element_type=F32)


def kernel(
    nz, nx, rows_dev, columns,
    patches, offsets, w_scale, w_rows, nodes, node_edges, own_nodes, t_rows, t_forward, t_back, t_last,
    surfaces, targets_out, positions_out, rms_out,
    arrived, spec_re, spec_im, staged, taps, met, sent_msg, gathered, all_nodes, ghosts,
    vec, weight, grams, mine,
    p_send, p_recv, n_send, n_recv, t_send, t_recv, g_send, g_recv, o_sem,
):
    z = lax.axis_index("gz")
    x = lax.axis_index("xy")
    length = patches.shape[-1]
    tiles = patches.shape[0]
    chunks = tiles // GROUP
    half_rows = nodes.shape[0] // 2
    high = half_rows + 2 * GHOST
    wide = nodes.shape[1]

    barrier = pltpu.get_barrier_semaphore()

    @pl.loop(0, nz)
    def _(zz):
        for xx in range(nx):
            @pl.when(jnp.logical_or(zz != z, x != xx))
            def _():
                pl.semaphore_signal(barrier, inc=1, device_id=(zz, xx), device_id_type=MESH)

    pl.semaphore_wait(barrier, nz * nx - 1)

    def chunk_ref(ref, c):
        return ref.at[pl.ds(c * GROUP, GROUP)]

    def patch_copy(d, c):
        source = chunk_ref(patches, c) if d == 0 else chunk_ref(arrived.at[d - 1], c)
        return pltpu.make_async_remote_copy(
            src_ref=source,
            dst_ref=chunk_ref(arrived.at[d], c),
            send_sem=p_send.at[d, c],
            recv_sem=p_recv.at[d, c],
            device_id=(jnp.maximum(z - 1, 0), x),
            device_id_type=MESH,
        )

    @pl.when(z > 0)
    def _():
        @pl.loop(0, chunks)
        def _(c):
            patch_copy(0, c).start()

    def fan(sources, targets, send, recv, act):
        @pl.loop(0, nz)
        def _(zz):
            for slot, test, xx in (
                (1, zz != z, x),
                (0, x + 1 < nx, jnp.minimum(x + 1, nx - 1)),
                (2, x > 0, jnp.maximum(x - 1, 0)),
            ):
                @pl.when(test)
                def _():
                    copy = pltpu.make_async_remote_copy(
                        src_ref=sources[slot],
                        dst_ref=targets[slot].at[z],
                        send_sem=send.at[slot, zz],
                        recv_sem=recv.at[slot, z],
                        device_id=(zz, xx),
                        device_id_type=MESH,
                    )
                    if act == "start":
                        copy.start()
                    else:
                        copy.wait_send()

    def fan_wait(sources, targets, send, recv):
        @pl.loop(0, nz)
        def _(zz):
            for slot, test, xx in ((1, zz != z, x), (0, x > 0, x), (2, x + 1 < nx, x)):
                @pl.when(test)
                def _():
                    pltpu.make_async_remote_copy(
                        src_ref=sources[slot],
                        dst_ref=targets[slot].at[zz],
                        send_sem=send.at[slot, zz],
                        recv_sem=recv.at[slot, zz],
                        device_id=(zz, xx),
                        device_id_type=MESH,
                    ).wait_recv()

    node_from = (node_edges.at[1], nodes, node_edges.at[0])
    node_to = (ghosts.at[0], all_nodes, ghosts.at[1])
    fan(node_from, node_to, n_send, n_recv, "start")

    def spectra(block):
        lines = dot(block.reshape(GROUP * length, length), t_rows[...]).astype(BF16)
        found = []
        for t in range(GROUP):
            one = lines[t * length : (t + 1) * length]
            pair = jnp.concatenate([one[:, :length], one[:, length:]], axis=0)
            both = dot(t_forward[...], pair)
            found.append((both[:length], both[length:]))
        return found

    @pl.loop(0, chunks)
    def _(c):
        for t, (real, imag) in enumerate(spectra(patches[pl.ds(c * GROUP, GROUP)])):
            spec_re[c * GROUP + t] = real
            spec_im[c * GROUP + t] = imag

    row_at = lax.broadcasted_iota(jnp.int32, (16, length), 0)
    row_at = jnp.where(row_at < 8, row_at, row_at - 16)
    col_at = lax.broadcasted_iota(jnp.int32, (1, length), 1)
    col_at = jnp.where(col_at < length // 2, col_at, col_at - length)

    for d in range(1, REACH + 1):
        live = z + d < nz

        @pl.when(jnp.logical_not(live))
        def _():
            arrived[d - 1] = jnp.zeros(arrived.shape[1:], arrived.dtype)

        @pl.loop(0, chunks)
        def _(c):
            @pl.when(live)
            def _():
                patch_copy(d - 1, c).wait_recv()

            if d < REACH:
                @pl.when(jnp.logical_and(live, z > 0))
                def _():
                    patch_copy(d, c).start()

            cross = []
            for t, (real, imag) in enumerate(spectra(arrived[d - 1, pl.ds(c * GROUP, GROUP)])):
                own_re = spec_re[c * GROUP + t]
                own_im = spec_im[c * GROUP + t]
                cross_re = (own_re * real + own_im * imag).astype(BF16)
                cross_im = (own_re * imag - own_im * real).astype(BF16)
                cross.append(jnp.concatenate([cross_re, cross_im], axis=1))
            half = dot(jnp.concatenate(cross, axis=0), t_back[...]).astype(BF16)
            for t in range(GROUP):
                tile = c * GROUP + t
                one = half[t * length : (t + 1) * length]
                pair = jnp.concatenate([one[:, :length], one[:, length:]], axis=0)
                corr = dot(t_last[...], pair) * (1.0 / float(length * length))
                staged[d - 1, tile] = corr.astype(BF16)
                near = jnp.concatenate([corr[:8], corr[length - 8 :]], axis=0)
                shift_row = offsets[2 * d - 2, pl.ds(tile, 1)]
                shift_col = offsets[2 * d - 1, pl.ds(tile, 1)]
                lines = [
                    jnp.sum(jnp.where(row_at == shift_row + s, near, 0.0), axis=0, keepdims=True)
                    for s in (-1, 0, 1)
                ]
                here = col_at == shift_col
                for s in range(3):
                    taps[s, d - 1, pl.ds(tile, 1)] = jnp.where(here, lines[s], 0.0)
                taps[3, d - 1, pl.ds(tile, 1)] = jnp.where(col_at == shift_col - 1, lines[1], 0.0)
                taps[4, d - 1, pl.ds(tile, 1)] = jnp.where(col_at == shift_col + 1, lines[1], 0.0)
            pltpu.make_async_copy(
                chunk_ref(staged.at[d - 1], c), chunk_ref(surfaces.at[d - 1], c), o_sem.at[d - 1, c]
            ).start()

    lane_tile = lax.broadcasted_iota(jnp.int32, (tiles, 128), 1)
    row_tile = lax.broadcasted_iota(jnp.int32, (tiles, 128), 0)
    level = floor_ratio * length
    lines = []
    for d in range(REACH):
        value = [jnp.sum(taps[s, d], axis=1, keepdims=True) for s in range(5)]
        for axis, (low, mid, top) in enumerate(((0, 1, 2), (3, 1, 4))):
            low, mid, top = value[low], value[mid], value[top]
            size = jnp.maximum(jnp.abs(low) + jnp.abs(mid) + jnp.abs(top), level)
            found = offsets[2 * d + axis].astype(F32) + (top - low) / size
            lines.append(
                jnp.sum(jnp.where(lane_tile == row_tile, found, 0.0), axis=0, keepdims=True)
            )
    message = jnp.concatenate(lines + [jnp.zeros((8 - 2 * REACH, 128), F32)], axis=0)
    targets_out[...] = message
    message = message * w_scale[...] + w_rows[...]
    sent_msg[...] = message
    gathered[1, z] = message
    message_from = (sent_msg, sent_msg, sent_msg)
    message_to = (gathered.at[0], gathered.at[1], gathered.at[2])
    fan(message_from, message_to, t_send, t_recv, "start")

    fan_wait(node_from, node_to, n_send, n_recv)
    all_nodes[z] = nodes[...]

    @pl.when(x == 0)
    def _():
        ghosts[0] = jnp.zeros(ghosts.shape[1:], ghosts.dtype)
        gathered[0] = jnp.zeros(gathered.shape[1:], gathered.dtype)

    @pl.when(x == nx - 1)
    def _():
        ghosts[1] = jnp.zeros(ghosts.shape[1:], ghosts.dtype)
        gathered[2] = jnp.zeros(gathered.shape[1:], gathered.dtype)

    for i in range(ITERS):
        for part in range(2):
            for pad in range(REACH):
                vec[i, part, pad] = jnp.zeros((high, wide), F32)
                vec[i, part, nz + REACH + pad] = jnp.zeros((high, wide), F32)
    for k in range(REACH):
        for pad in range(REACH):
            weight[k, pad] = jnp.zeros((high, wide), F32)

    @pl.loop(0, nz)
    def _(zz):
        body = all_nodes[zz].astype(F32)
        above = ghosts[0, zz].astype(F32)
        below = ghosts[1, zz].astype(F32)
        for part in range(2):
            vec[0, part, zz + REACH, pl.ds(0, GHOST)] = above[part * GHOST : (part + 1) * GHOST]
            vec[0, part, zz + REACH, pl.ds(GHOST, half_rows)] = body[
                part * half_rows : (part + 1) * half_rows
            ]
            vec[0, part, zz + REACH, pl.ds(GHOST + half_rows, GHOST)] = below[
                part * GHOST : (part + 1) * GHOST
            ]

    fan_wait(message_from, message_to, t_send, t_recv)

    pick_from = lax.broadcasted_iota(jnp.int32, (128, wide), 0)
    pick_to = lax.broadcasted_iota(jnp.int32, (128, wide), 1) // SUB

    def spread(slot, line, base):
        pick = (pick_from == pick_to + (base + line * columns)).astype(F32)
        return jnp.dot(
            gathered[slot].reshape(nz * 8, 128), pick,
            precision=lax.Precision.HIGHEST, preferred_element_type=F32,
        )

    pieces = (
        [(0, rows_dev - 1, 0, GHOST)]
        + [(1, r, GHOST + r * SUB, SUB) for r in range(rows_dev)]
        + [(2, 0, GHOST + half_rows, GHOST)]
    )
    for slot, line, start, count in pieces:
        met[0] = spread(slot, line, 0)
        met[1] = spread(slot, line, rows_dev * columns)

        @pl.loop(0, nz)
        def _(zz):
            for k in range(REACH):
                weight[k, zz + REACH, pl.ds(start, count)] = jnp.broadcast_to(
                    met[1, pl.ds(zz * 8 + k, 1)], (count, wide)
                )
            for part in range(2):
                total = jnp.zeros((1, wide), F32)
                for k in range(REACH):
                    here = met[0, pl.ds(zz * 8 + 2 * k + part, 1)]
                    behind = jnp.maximum(zz - k - 1, 0)
                    back = met[0, pl.ds(behind * 8 + 2 * k + part, 1)]
                    total = total - here + jnp.where(zz > k, back, 0.0)
                vec[ITERS, part, zz + REACH, pl.ds(start, count)] = jnp.broadcast_to(
                    total, (count, wide)
                )

    row_id = lax.broadcasted_iota(jnp.int32, (high, wide), 0)
    col_id = lax.broadcasted_iota(jnp.int32, (high, wide), 1)
    first = jnp.logical_and(row_id == GHOST, x == 0)
    final = jnp.logical_and(row_id == GHOST + half_rows - 1, x == nx - 1)

    def apply(source, target, extra):
        @pl.loop(0, nz)
        def _(zz):
            at = zz + REACH
            for part in range(2):
                v = vec[source, part, at]
                up = jnp.where(first, v, pltpu.roll(v, 1, 0))
                down = jnp.where(final, v, pltpu.roll(v, high - 1, 0))
                left = jnp.where(col_id == 0, v, pltpu.roll(v, 1, 1))
                right = jnp.where(col_id == wide - 1, v, pltpu.roll(v, wide - 1, 1))
                force = lattice_stiff * (up + down + left + right - 4.0 * v)
                if extra is not None:
                    force = force + vec[extra, part, at]
                for k in range(1, REACH + 1):
                    force = force + weight[k - 1, at] * (vec[source, part, at + k] - v)
                    force = force - weight[k - 1, at - k] * (v - vec[source, part, at - k])
                vec[target, part, at] = force

    apply(0, 1, ITERS)
    for i in range(1, ITERS):
        apply(i, i + 1, None)

    pairs = [(i, j) for i in range(ITERS) for j in range(i, ITERS)]

    def products(zz, held):
        held = list(held)
        for part in range(2):
            values = [
                vec[i + 1, part, zz + REACH, pl.ds(GHOST, half_rows)].reshape(
                    half_rows // 8, 8, wide
                )
                for i in range(ITERS)
            ]
            for n, (i, j) in enumerate(pairs):
                held[n] = held[n] + jnp.sum(values[i] * values[j], axis=0)
        return tuple(held)

    held = lax.fori_loop(0, nz, products, tuple(jnp.zeros((8, wide), F32) for _ in pairs))
    lane = lax.broadcasted_iota(jnp.int32, (8, 128), 1)
    gram = jnp.zeros((8, 128), F32)
    for n in range(len(pairs)):
        line = jnp.sum(held[n], axis=0, keepdims=True)
        gram = jnp.where(lane == n, jnp.sum(line, axis=1, keepdims=True), gram)
    mine[...] = gram
    grams[x] = gram

    def gram_copy(xx, where):
        return pltpu.make_async_remote_copy(
            src_ref=mine,
            dst_ref=grams.at[where],
            send_sem=g_send.at[xx],
            recv_sem=g_recv.at[where],
            device_id=(z, xx),
            device_id_type=MESH,
        )

    for xx in range(nx):
        @pl.when(xx != x)
        def _():
            gram_copy(xx, x).start()
    for xx in range(nx):
        @pl.when(xx != x)
        def _():
            gram_copy(xx, xx).wait_recv()
    total = grams[0]
    for xx in range(1, nx):
        total = total + grams[xx]
    total = total[:1]
    lane = lax.broadcasted_iota(jnp.int32, (1, 128), 1)
    inner = {}
    for n, (i, j) in enumerate(pairs):
        inner[i, j] = jnp.sum(jnp.where(lane == n, total, 0.0), axis=1, keepdims=True)
        inner[j, i] = inner[i, j]
    count = 2.0 * nz * nx * half_rows * wide
    factors = [jnp.ones((1, 1), F32)]
    moved = [jnp.zeros((1, 1), F32) for _ in range(ITERS)]
    report = jnp.zeros((1, 128), F32)
    for i in range(ITERS):
        size = jnp.zeros((1, 1), F32)
        for a in range(i + 1):
            for b in range(i + 1):
                size = size + factors[a] * factors[b] * inner[a, b]
        rms = jnp.sqrt(jnp.maximum(size, 0.0) / count + tiny_eps)
        report = jnp.where(lane == i, rms, report)
        step = step_size * jnp.minimum(1.0, clip_level / rms)
        for a in range(i + 1):
            moved[a] = moved[a] + step * factors[a]
        later = factors + [jnp.zeros((1, 1), F32)]
        for a in range(i + 1):
            later[a + 1] = later[a + 1] + step * factors[a]
        factors = later
    rms_out[...] = report
    for part in range(2):
        result = own_nodes[part]
        for i in range(ITERS):
            result = result + moved[i] * vec[i + 1, part, z + REACH, pl.ds(GHOST, half_rows)]
        positions_out[part] = result

    for xx in range(nx):
        @pl.when(xx != x)
        def _():
            gram_copy(xx, x).wait_send()
    fan(node_from, node_to, n_send, n_recv, "wait")
    fan(message_from, message_to, t_send, t_recv, "wait")
    for d in range(REACH):
        @pl.when(jnp.logical_and(z > 0, z + d < nz))
        def _():
            @pl.loop(0, chunks)
            def _(c):
                patch_copy(d, c).wait_send()

        @pl.loop(0, chunks)
        def _(c):
            pltpu.make_async_copy(
                chunk_ref(staged.at[d], c), chunk_ref(surfaces.at[d], c), o_sem.at[d, c]
            ).wait()


def local(nz, nx, patches, peak_offsets, valid_masks, initial_positions):
    length = patches.shape[-1]
    rows_dev, columns = patches.shape[1:3]
    tiles = rows_dev * columns
    chunks = tiles // GROUP
    half_rows, wide = initial_positions.shape[2:]
    high = half_rows + 2 * GHOST
    z = lax.axis_index("gz")
    offsets = jnp.broadcast_to(peak_offsets.reshape(2 * REACH, tiles, 1), (2 * REACH, tiles, 128))
    reach = jnp.arange(1, REACH + 1)
    live = jnp.where(z + reach < nz, 1.0 / reach.astype(F32), 0.0)
    weights = valid_masks.reshape(REACH, tiles).astype(F32) * live[:, None]
    scale = jnp.pad(jnp.repeat(weights, 2, axis=0), ((0, 8 - 2 * REACH), (0, 128 - tiles)))
    lines = jnp.pad(weights, ((0, 8 - REACH), (tiles, 128 - 2 * tiles)))
    own = initial_positions[:, 0]
    narrow = own.astype(BF16)
    edges = jnp.stack([narrow[:, :GHOST], narrow[:, -GHOST:]]).reshape(2, 2 * GHOST, wide)
    vmem = pl.BlockSpec(memory_space=pltpu.VMEM)
    surfaces, targets, positions, rms = pl.pallas_call(
        functools.partial(kernel, nz, nx, rows_dev, columns),
        out_shape=(
            jax.ShapeDtypeStruct((REACH, tiles, length, length), BF16),
            jax.ShapeDtypeStruct((8, 128), F32),
            jax.ShapeDtypeStruct((2, half_rows, wide), F32),
            jax.ShapeDtypeStruct((1, 128), F32),
        ),
        in_specs=[vmem] * 11,
        out_specs=(pl.BlockSpec(memory_space=pl.ANY), vmem, vmem, vmem),
        scratch_shapes=[
            pltpu.VMEM((REACH, tiles, length, length), BF16),
            pltpu.VMEM((tiles, length, length), F32),
            pltpu.VMEM((tiles, length, length), F32),
            pltpu.VMEM((REACH, tiles, length, length), BF16),
            pltpu.VMEM((5, REACH, tiles, 128), F32),
            pltpu.VMEM((2, nz * 8, wide), F32),
            pltpu.VMEM((8, 128), F32),
            pltpu.VMEM((3, nz, 8, 128), F32),
            pltpu.VMEM((nz, 2 * half_rows, wide), BF16),
            pltpu.VMEM((2, nz, 2 * GHOST, wide), BF16),
            pltpu.VMEM((ITERS + 1, 2, nz + 2 * REACH, high, wide), F32),
            pltpu.VMEM((REACH, nz + REACH, high, wide), F32),
            pltpu.VMEM((nx, 8, 128), F32),
            pltpu.VMEM((8, 128), F32),
            pltpu.SemaphoreType.DMA((REACH, chunks)),
            pltpu.SemaphoreType.DMA((REACH, chunks)),
            pltpu.SemaphoreType.DMA((3, nz)),
            pltpu.SemaphoreType.DMA((3, nz)),
            pltpu.SemaphoreType.DMA((3, nz)),
            pltpu.SemaphoreType.DMA((3, nz)),
            pltpu.SemaphoreType.DMA((nx,)),
            pltpu.SemaphoreType.DMA((nx,)),
            pltpu.SemaphoreType.DMA((REACH, chunks)),
        ],
        compiler_params=pltpu.CompilerParams(
            collective_id=0, has_side_effects=True, vmem_limit_bytes=67043328
        ),
        name="align",
    )(
        patches.reshape(tiles, length, length), offsets, scale, lines,
        narrow.reshape(2 * half_rows, wide), edges, own, *tables(length),
    )
    return (
        positions[:, None],
        targets[: 2 * REACH, :tiles].reshape(1, 2 * REACH, rows_dev, columns),
        surfaces.reshape(1, REACH, rows_dev, columns, length, length),
        rms[0, :ITERS],
    )


def solution(mesh):
    in_specs = (
        P("gz", "xy", None, None, None),
        P("gz", None, "xy", None),
        P("gz", None, "xy", None),
        P(None, "gz", "xy", None),
    )
    out_specs = (
        P(None, "gz", "xy", None),
        P("gz", None, "xy", None),
        P("gz", None, "xy", None, None, None),
        P(),
    )
    body = functools.partial(local, mesh.shape["gz"], mesh.shape["xy"])
    return jax.shard_map(body, mesh=mesh, in_specs=in_specs, out_specs=out_specs, check_vma=False)
```

time: 439 us -> 80.6 us (0.18); the launches traced: 433 us -> 80.2 us
  blocking collectives: 178 us -> 0 us
  starting transfers between devices: 130 us -> 0 us
  matrix products: 79.1 us -> 0 us
  Pallas kernels: 0 us -> 65.9 us
  other arithmetic: 14 us -> 2.91 us
  waiting for transfers between devices: 8.73 us -> 0 us
  local copies, waits for them, and re-layouts: 18.3 us -> 10.8 us
  between operations: 5.25 us -> 0.65 us
    psum x4 -> x0, blocking collectives: 178 us -> none  [local(): total = lax.psum(jnp.sum(force * force), ('gz', 'xy'))]
    ppermute x41 -> x0, starting transfers between devices: 130 us -> none  [the longest x33 113 us: from_behind(): return lax.ppermute(array, axis, pairs)]
    dot_general x42 -> x0, matrix products: 79.1 us -> none  [the longest x22 44.1 us: left_product(): jnp.einsum('ja,pak->pjk', table, right, preferred_element_type=jnp.float32)]
    pallas_call x0 -> x1, Pallas kernels: none -> 65.9 us  [local(): pl.pallas_call(functools.partial(kernel, nz, nx, rows_dev, columns), out_...]
    ppermute x41 -> x0, waiting for transfers between devices: 8.73 us -> none  [the longest x33 5 us: from_behind(): return lax.ppermute(array, axis, pairs)]
    slice x25 -> x0, local copies, waits for them, and re-layouts: 5.01 us -> none  [the longest x6 1.83 us: refine(): along_rows = values[:, :, 1]]
  transfers between devices with their start and end apart: 41 -> 0, of which waited for: 7 -> 0; matrix products, arithmetic and copies ran while one was open for 24% -> 0% of each run, Pallas kernels for 0% -> 0%
where the time goes in v1:
time: 80.6 us; the launch traced here: 80.2 us
  Pallas kernels  65.9 us (82%)
  local copies, waits for them, and re-layouts  10.8 us (13%)
  other arithmetic  2.91 us (4%)
    pallas_call x1, Pallas kernels, local(): pl.pallas_call(functools.partial(kernel, nz, nx, rows_dev, columns), out_...  65.9 us
    unnamed x2, local copies, waits for them, and re-layouts  5.44 us

profile of v1, /device:TPU:0, one launch (start us, length us, event | category | flops | bytes accessed | tf_op | source)
XLA Modules:
  0.0 80.2 jit_solution(16226113444497593475)
XLA Ops:
  0.6 1.5 %bitcast_convert_fusion = (bf16[2,32,256]{2,1,0:T(8,128)(2,1)S(1)}, bf16[2,1,32,256]{3,2,1,0:T(8,128)(2,1)}) fusion(f32[2,1,32,256]{3,2,1,0:T(8,128)} %param.11), kind=kLoop, calls=%fused_computation.6 | loop fusion | flops 32768 | bytes 131072 | tf_op jit(solution)/shard_map/convert_element_type | solution.py:438
  2.2 0.6 pad_maximum_fusion.node_edges
  2.8 0.7 convert_element_type.26
  3.5 0.1 convert_element_type.27
  3.6 0.1 broadcast_multiply_fusion
  3.6 0.6 pad.8.w_scale
  4.3 0.7 pad.9.w_rows
  4.9 0.8 broadcast_in_dim.18
  5.7 0.7 broadcast_in_dim.19.offsets
  6.4 65.9 %align.1 = (bf16[3,32,128,128]{3,2,1,0:T(8,128)(2,1)}, f32[8,128]{1,0:T(8,128)}, f32[2,32,256]{2,1,0:T(8,128)}, f32[1,128]{1,0:T(1,128)}) custom-call(bf16[32,128,128]{2,1,0:T(8,128)(2,1)} %bitcast.16, s32[6,32,128]{2,1,0:T(8,128)} %broadcast_in_dim.19.offsets, f32[8,128]{1,0:T(8,128)} %pad.8.w_scale, f32[8,128]{1,0:T(8,128)} %pad.9.w_rows, ...), custom_call_target="tpu_custom_call" | custom-call | tf_op jit(solution)/shard_map/align/pallas_call | solution.py:441
  72.3 1.3 %reshape.43 = f32[1,6,2,16]{3,2,1,0:T(2,128)} reshape(f32[6,32]{1,0:T(8,128)} %bitcast.20) | data formatting | bytes 1536 | tf_op jit(solution)/shard_map/reshape | solution.py:486
  73.6 1.2 %slice_bitcast_fusion.2 = f32[4]{0:T(128)} fusion(f32[1,128]{1,0:T(1,128)} %get-tuple-element.11), kind=kLoop, calls=%fused_computation.5 | loop fusion | bytes 32 | tf_op jit(solution)/shard_map/squeeze | solution.py:488
  74.8 1.5 %copy.15 = f32[2,1,32,256]{3,2,1,0:T(8,128)} copy(f32[2,1,32,256]{3,2,1,0:T(8,128)} %bitcast.19) | data formatting | bytes 131072
  76.3 4.0 %copy.16 = bf16[1,3,2,16,128,128]{5,4,3,2,1,0:T(8,128)(2,1)} copy(bf16[1,3,2,16,128,128]{5,4,3,2,1,0:T(8,128)(2,1)} %bitcast.15) | data formatting | bytes 6291456
  (4 shorter events, 0.0 us)

commit v2 on v1

--- a/solution.py
+++ b/solution.py
@@ -44,11 +44,11 @@
 
 def kernel(
     nz, nx, rows_dev, columns,
-    patches, offsets, w_scale, w_rows, nodes, node_edges, own_nodes, t_rows, t_forward, t_back, t_last,
+    patches, peaks, masks, own_nodes, t_rows, t_forward, t_back, t_last,
     surfaces, targets_out, positions_out, rms_out,
-    arrived, spec_re, spec_im, staged, taps, met, sent_msg, gathered, all_nodes, ghosts,
+    arrived, spec_re, spec_im, offsets, trust, nodes, node_edges, taps, met, sent_msg, gathered, all_nodes, ghosts,
     vec, weight, grams, mine,
-    p_send, p_recv, n_send, n_recv, t_send, t_recv, g_send, g_recv, o_sem,
+    p_send, p_recv, n_send, n_recv, t_send, t_recv, g_send, g_recv,
 ):
     z = lax.axis_index("gz")
     x = lax.axis_index("xy")
@@ -68,27 +68,78 @@
             def _():
                 pl.semaphore_signal(barrier, inc=1, device_id=(zz, xx), device_id_type=MESH)
 
+    narrow = own_nodes[...].astype(BF16)
+    for part in range(2):
+        base = part * half_rows
+        nodes[pl.ds(base, half_rows)] = narrow[part]
+    node_edges[0] = jnp.concatenate([narrow[part, :GHOST] for part in range(2)], axis=0)
+    node_edges[1] = jnp.concatenate([narrow[part, half_rows - GHOST :] for part in range(2)], axis=0)
+    across = lax.broadcasted_iota(jnp.int32, (columns, columns), 1)
+    along = lax.broadcasted_iota(jnp.int32, (columns, columns), 0)
+
+    def upright(line):
+        return jnp.sum(jnp.where(across == along, line, 0), axis=1, keepdims=True)
+
+    for r in range(rows_dev):
+        here = pl.ds(r * columns, columns)
+        for q in range(2 * REACH):
+            offsets[q, here] = jnp.broadcast_to(upright(peaks[q, r : r + 1, :]), (columns, 128))
+        for k in range(REACH):
+            share = jnp.where(z + k + 1 < nz, 1.0 / (k + 1), 0.0)
+            trust[k, here] = jnp.broadcast_to(
+                upright(masks[k, r : r + 1, :]).astype(F32) * share, (columns, 128)
+            )
+
+    for i in range(ITERS):
+        for part in range(2):
+            for pad in range(REACH):
+                vec[i, part, pad] = jnp.zeros((high, wide), F32)
+                vec[i, part, nz + REACH + pad] = jnp.zeros((high, wide), F32)
+    for k in range(REACH):
+        for pad in range(REACH):
+            weight[k, pad] = jnp.zeros((high, wide), F32)
+
     pl.semaphore_wait(barrier, nz * nx - 1)
 
     def chunk_ref(ref, c):
         return ref.at[pl.ds(c * GROUP, GROUP)]
 
-    def patch_copy(d, c):
-        source = chunk_ref(patches, c) if d == 0 else chunk_ref(arrived.at[d - 1], c)
+    def own_copy(kind, c):
+        slot = 2 * kind
         return pltpu.make_async_remote_copy(
-            src_ref=source,
-            dst_ref=chunk_ref(arrived.at[d], c),
-            send_sem=p_send.at[d, c],
-            recv_sem=p_recv.at[d, c],
-            device_id=(jnp.maximum(z - 1, 0), x),
+            src_ref=chunk_ref(patches, c),
+            dst_ref=chunk_ref(arrived.at[slot], c),
+            send_sem=p_send.at[kind, c],
+            recv_sem=p_recv.at[slot, c],
+            device_id=(z - 1 - slot, x),
             device_id_type=MESH,
         )
 
-    @pl.when(z > 0)
-    def _():
-        @pl.loop(0, chunks)
-        def _(c):
-            patch_copy(0, c).start()
+    def passed_copy(slot, c):
+        later = (slot + 1) % 3
+        return pltpu.make_async_remote_copy(
+            src_ref=chunk_ref(arrived.at[slot], c),
+            dst_ref=chunk_ref(arrived.at[later], c),
+            send_sem=p_send.at[slot + 2, c],
+            recv_sem=p_recv.at[later, c],
+            device_id=(z - 1 + 3 * ((slot + 1) // 3), x),
+            device_id_type=MESH,
+        )
+
+    own_tests = (z % 4 != 0, jnp.logical_and(z % 2 == 0, z >= 4))
+
+    def passes(slot):
+        one = jnp.logical_and(slot == 0, z > 0)
+        two = jnp.logical_and(slot == 1, z % 2 == 1)
+        three = jnp.logical_and(slot == 2, jnp.logical_and(z % 4 == 1, z + 2 < nz))
+        return jnp.logical_and(jnp.logical_or(one, jnp.logical_or(two, three)), z + slot + 1 < nz)
+
+    @pl.loop(0, chunks)
+    def _(c):
+        for kind in range(2):
+            @pl.when(own_tests[kind])
+            def _():
+                own_copy(kind, c).start()
 
     def fan(sources, targets, send, recv, act):
         @pl.loop(0, nz)
@@ -153,53 +204,63 @@
     col_at = lax.broadcasted_iota(jnp.int32, (1, length), 1)
     col_at = jnp.where(col_at < length // 2, col_at, col_at - length)
 
-    for d in range(1, REACH + 1):
-        live = z + d < nz
-
-        @pl.when(jnp.logical_not(live))
+    for slot in range(REACH):
+        @pl.when(z + slot + 1 >= nz)
         def _():
-            arrived[d - 1] = jnp.zeros(arrived.shape[1:], arrived.dtype)
-
-        @pl.loop(0, chunks)
-        def _(c):
-            @pl.when(live)
-            def _():
-                patch_copy(d - 1, c).wait_recv()
-
-            if d < REACH:
-                @pl.when(jnp.logical_and(live, z > 0))
-                def _():
-                    patch_copy(d, c).start()
-
-            cross = []
-            for t, (real, imag) in enumerate(spectra(arrived[d - 1, pl.ds(c * GROUP, GROUP)])):
-                own_re = spec_re[c * GROUP + t]
-                own_im = spec_im[c * GROUP + t]
-                cross_re = (own_re * real + own_im * imag).astype(BF16)
-                cross_im = (own_re * imag - own_im * real).astype(BF16)
-                cross.append(jnp.concatenate([cross_re, cross_im], axis=1))
-            half = dot(jnp.concatenate(cross, axis=0), t_back[...]).astype(BF16)
-            for t in range(GROUP):
-                tile = c * GROUP + t
-                one = half[t * length : (t + 1) * length]
-                pair = jnp.concatenate([one[:, :length], one[:, length:]], axis=0)
-                corr = dot(t_last[...], pair) * (1.0 / float(length * length))
-                staged[d - 1, tile] = corr.astype(BF16)
-                near = jnp.concatenate([corr[:8], corr[length - 8 :]], axis=0)
-                shift_row = offsets[2 * d - 2, pl.ds(tile, 1)]
-                shift_col = offsets[2 * d - 1, pl.ds(tile, 1)]
-                lines = [
-                    jnp.sum(jnp.where(row_at == shift_row + s, near, 0.0), axis=0, keepdims=True)
-                    for s in (-1, 0, 1)
-                ]
-                here = col_at == shift_col
-                for s in range(3):
-                    taps[s, d - 1, pl.ds(tile, 1)] = jnp.where(here, lines[s], 0.0)
-                taps[3, d - 1, pl.ds(tile, 1)] = jnp.where(col_at == shift_col - 1, lines[1], 0.0)
-                taps[4, d - 1, pl.ds(tile, 1)] = jnp.where(col_at == shift_col + 1, lines[1], 0.0)
-            pltpu.make_async_copy(
-                chunk_ref(staged.at[d - 1], c), chunk_ref(surfaces.at[d - 1], c), o_sem.at[d - 1, c]
-            ).start()
+            arrived[slot] = jnp.zeros(arrived.shape[1:], arrived.dtype)
+
+    even = 1 - z % 2
+    three = (z % 2) * ((z % 4) // 2)
+    one = 1 - even - three
+
+    @pl.loop(0, REACH * chunks)
+    def _(n):
+        ended = n // (2 * chunks)
+        slot = (
+            even * (n // chunks)
+            + one * ((1 - ended) * (n % 2) * 2 + ended)
+            + three * (n % 3)
+        )
+        c = (
+            even * (n % chunks)
+            + one * ((1 - ended) * (n // 2) + ended * (n - 2 * chunks))
+            + three * (n // 3)
+        )
+
+        @pl.when(z + slot + 1 < nz)
+        def _():
+            passed_copy((slot + 2) % 3, c).wait_recv()
+
+        @pl.when(passes(slot))
+        def _():
+            passed_copy(slot, c).start()
+
+        cross = []
+        for t, (real, imag) in enumerate(spectra(arrived[slot, pl.ds(c * GROUP, GROUP)])):
+            own_re = spec_re[c * GROUP + t]
+            own_im = spec_im[c * GROUP + t]
+            cross_re = (own_re * real + own_im * imag).astype(BF16)
+            cross_im = (own_re * imag - own_im * real).astype(BF16)
+            cross.append(jnp.concatenate([cross_re, cross_im], axis=1))
+        half = dot(jnp.concatenate(cross, axis=0), t_back[...]).astype(BF16)
+        for t in range(GROUP):
+            tile = c * GROUP + t
+            block = half[t * length : (t + 1) * length]
+            pair = jnp.concatenate([block[:, :length], block[:, length:]], axis=0)
+            corr = dot(t_last[...], pair) * (1.0 / float(length * length))
+            surfaces[slot, tile] = corr.astype(BF16)
+            near = jnp.concatenate([corr[:8], corr[length - 8 :]], axis=0)
+            shift_row = offsets[2 * slot, pl.ds(tile, 1)]
+            shift_col = offsets[2 * slot + 1, pl.ds(tile, 1)]
+            lines = [
+                jnp.sum(jnp.where(row_at == shift_row + s, near, 0.0), axis=0, keepdims=True)
+                for s in (-1, 0, 1)
+            ]
+            here = col_at == shift_col
+            for s in range(3):
+                taps[s, slot, pl.ds(tile, 1)] = jnp.where(here, lines[s], 0.0)
+            taps[3, slot, pl.ds(tile, 1)] = jnp.where(col_at == shift_col - 1, lines[1], 0.0)
+            taps[4, slot, pl.ds(tile, 1)] = jnp.where(col_at == shift_col + 1, lines[1], 0.0)
 
     lane_tile = lax.broadcasted_iota(jnp.int32, (tiles, 128), 1)
     row_tile = lax.broadcasted_iota(jnp.int32, (tiles, 128), 0)
@@ -211,12 +272,17 @@
             low, mid, top = value[low], value[mid], value[top]
             size = jnp.maximum(jnp.abs(low) + jnp.abs(mid) + jnp.abs(top), level)
             found = offsets[2 * d + axis].astype(F32) + (top - low) / size
-            lines.append(
-                jnp.sum(jnp.where(lane_tile == row_tile, found, 0.0), axis=0, keepdims=True)
-            )
+            for r in range(rows_dev):
+                block = found[r * columns : (r + 1) * columns, :columns]
+                targets_out[2 * d + axis, r : r + 1, :] = jnp.sum(
+                    jnp.where(across == along, block, 0.0), axis=0, keepdims=True
+                )
+            line = jnp.where(lane_tile == row_tile, found * trust[d], 0.0)
+            lines.append(line)
+    for k in range(REACH):
+        lines[k] = lines[k] + jnp.where(lane_tile == row_tile + tiles, trust[k], 0.0)
+    lines = [jnp.sum(line, axis=0, keepdims=True) for line in lines]
     message = jnp.concatenate(lines + [jnp.zeros((8 - 2 * REACH, 128), F32)], axis=0)
-    targets_out[...] = message
-    message = message * w_scale[...] + w_rows[...]
     sent_msg[...] = message
     gathered[1, z] = message
     message_from = (sent_msg, sent_msg, sent_msg)
@@ -235,15 +301,6 @@
     def _():
         ghosts[1] = jnp.zeros(ghosts.shape[1:], ghosts.dtype)
         gathered[2] = jnp.zeros(gathered.shape[1:], gathered.dtype)
-
-    for i in range(ITERS):
-        for part in range(2):
-            for pad in range(REACH):
-                vec[i, part, pad] = jnp.zeros((high, wide), F32)
-                vec[i, part, nz + REACH + pad] = jnp.zeros((high, wide), F32)
-    for k in range(REACH):
-        for pad in range(REACH):
-            weight[k, pad] = jnp.zeros((high, wide), F32)
 
     @pl.loop(0, nz)
     def _(zz):
@@ -393,7 +450,7 @@
         for a in range(i + 1):
             later[a + 1] = later[a + 1] + step * factors[a]
         factors = later
-    rms_out[...] = report
+    rms_out[...] = report[0, :ITERS]
     for part in range(2):
         result = own_nodes[part]
         for i in range(ITERS):
@@ -406,18 +463,36 @@
             gram_copy(xx, x).wait_send()
     fan(node_from, node_to, n_send, n_recv, "wait")
     fan(message_from, message_to, t_send, t_recv, "wait")
-    for d in range(REACH):
-        @pl.when(jnp.logical_and(z > 0, z + d < nz))
-        def _():
-            @pl.loop(0, chunks)
-            def _(c):
-                patch_copy(d, c).wait_send()
-
-        @pl.loop(0, chunks)
-        def _(c):
-            pltpu.make_async_copy(
-                chunk_ref(staged.at[d], c), chunk_ref(surfaces.at[d], c), o_sem.at[d, c]
-            ).wait()
+    @pl.loop(0, chunks)
+    def _(c):
+        for kind in range(2):
+            @pl.when(own_tests[kind])
+            def _():
+                own_copy(kind, c).wait_send()
+        for slot in range(REACH):
+            @pl.when(passes(slot))
+            def _():
+                passed_copy(slot, c).wait_send()
+
+
+def deliver(*refs):
+    held, out, sems = refs[:4], refs[4:8], refs[8]
+    copies = []
+    for n in range(4):
+        parts = held[n].shape[0] if n == 0 else 1
+        for part in range(parts):
+            at = pl.ds(part, 1) if n == 0 else slice(None)
+            copies.append(
+                pltpu.make_async_copy(
+                    held[n].at[at] if n == 0 else held[n],
+                    out[n].at[at] if n == 0 else out[n],
+                    sems.at[len(copies)],
+                )
+            )
+    for copy in copies:
+        copy.start()
+    for copy in copies:
+        copy.wait()
 
 
 def local(nz, nx, patches, peak_offsets, valid_masks, initial_positions):
@@ -427,32 +502,28 @@
     chunks = tiles // GROUP
     half_rows, wide = initial_positions.shape[2:]
     high = half_rows + 2 * GHOST
-    z = lax.axis_index("gz")
-    offsets = jnp.broadcast_to(peak_offsets.reshape(2 * REACH, tiles, 1), (2 * REACH, tiles, 128))
-    reach = jnp.arange(1, REACH + 1)
-    live = jnp.where(z + reach < nz, 1.0 / reach.astype(F32), 0.0)
-    weights = valid_masks.reshape(REACH, tiles).astype(F32) * live[:, None]
-    scale = jnp.pad(jnp.repeat(weights, 2, axis=0), ((0, 8 - 2 * REACH), (0, 128 - tiles)))
-    lines = jnp.pad(weights, ((0, 8 - REACH), (tiles, 128 - 2 * tiles)))
     own = initial_positions[:, 0]
-    narrow = own.astype(BF16)
-    edges = jnp.stack([narrow[:, :GHOST], narrow[:, -GHOST:]]).reshape(2, 2 * GHOST, wide)
+    grant = min(67043328, (36 << 20) + nz * (nz > 16) * (1 << 20))
     vmem = pl.BlockSpec(memory_space=pltpu.VMEM)
-    surfaces, targets, positions, rms = pl.pallas_call(
+    shapes = (
+        jax.ShapeDtypeStruct((REACH, tiles, length, length), BF16),
+        jax.ShapeDtypeStruct((2 * REACH, rows_dev, columns), F32),
+        jax.ShapeDtypeStruct((2, half_rows, wide), F32),
+        jax.ShapeDtypeStruct((ITERS,), F32),
+    )
+    held = pl.pallas_call(
         functools.partial(kernel, nz, nx, rows_dev, columns),
-        out_shape=(
-            jax.ShapeDtypeStruct((REACH, tiles, length, length), BF16),
-            jax.ShapeDtypeStruct((8, 128), F32),
-            jax.ShapeDtypeStruct((2, half_rows, wide), F32),
-            jax.ShapeDtypeStruct((1, 128), F32),
-        ),
-        in_specs=[vmem] * 11,
-        out_specs=(pl.BlockSpec(memory_space=pl.ANY), vmem, vmem, vmem),
+        out_shape=shapes,
+        in_specs=[vmem] * 8,
+        out_specs=(vmem,) * 4,
         scratch_shapes=[
             pltpu.VMEM((REACH, tiles, length, length), BF16),
             pltpu.VMEM((tiles, length, length), F32),
             pltpu.VMEM((tiles, length, length), F32),
-            pltpu.VMEM((REACH, tiles, length, length), BF16),
+            pltpu.VMEM((2 * REACH, tiles, 128), jnp.int32),
+            pltpu.VMEM((REACH, tiles, 128), F32),
+            pltpu.VMEM((2 * half_rows, wide), BF16),
+            pltpu.VMEM((2, 2 * GHOST, wide), BF16),
             pltpu.VMEM((5, REACH, tiles, 128), F32),
             pltpu.VMEM((2, nz * 8, wide), F32),
             pltpu.VMEM((8, 128), F32),
@@ -463,7 +534,7 @@
             pltpu.VMEM((REACH, nz + REACH, high, wide), F32),
             pltpu.VMEM((nx, 8, 128), F32),
             pltpu.VMEM((8, 128), F32),
-            pltpu.SemaphoreType.DMA((REACH, chunks)),
+            pltpu.SemaphoreType.DMA((REACH + 2, chunks)),
             pltpu.SemaphoreType.DMA((REACH, chunks)),
             pltpu.SemaphoreType.DMA((3, nz)),
             pltpu.SemaphoreType.DMA((3, nz)),
@@ -471,21 +542,28 @@
             pltpu.SemaphoreType.DMA((3, nz)),
             pltpu.SemaphoreType.DMA((nx,)),
             pltpu.SemaphoreType.DMA((nx,)),
-            pltpu.SemaphoreType.DMA((REACH, chunks)),
         ],
         compiler_params=pltpu.CompilerParams(
-            collective_id=0, has_side_effects=True, vmem_limit_bytes=67043328
+            collective_id=0, has_side_effects=True, vmem_limit_bytes=grant
         ),
         name="align",
     )(
-        patches.reshape(tiles, length, length), offsets, scale, lines,
-        narrow.reshape(2 * half_rows, wide), edges, own, *tables(length),
+        patches.reshape(tiles, length, length), peak_offsets[0], valid_masks[0], own, *tables(length)
     )
+    surfaces, targets, positions, rms = pl.pallas_call(
+        deliver,
+        out_shape=shapes,
+        in_specs=[vmem] * 4,
+        out_specs=(pl.BlockSpec(memory_space=pl.ANY),) * 4,
+        scratch_shapes=[pltpu.SemaphoreType.DMA((REACH + 3,))],
+        compiler_params=pltpu.CompilerParams(vmem_limit_bytes=8 << 20),
+        name="deliver",
+    )(*held)
     return (
         positions[:, None],
-        targets[: 2 * REACH, :tiles].reshape(1, 2 * REACH, rows_dev, columns),
+        targets[None],
         surfaces.reshape(1, REACH, rows_dev, columns, length, length),
-        rms[0, :ITERS],
+        rms,
     )
 
 

time: 80.6 us -> 72.5 us (0.90)
  local copies, waits for them, and re-layouts: 10.8 us -> 6.92 us
  other arithmetic: 2.91 us -> 0 us
  Pallas kernels: 65.9 us -> 64.5 us
    pallas_call x1, Pallas kernels: 65.9 us -> 62.8 us  [local(): pl.pallas_call(functools.partial(kernel, nz, nx, rows_dev, columns), out_...]
    convert_element_type x2 -> x0, other arithmetic: 2.22 us -> none  [the longest x1 1.54 us: local(): narrow = own.astype(BF16)]
    pallas_call x0 -> x1, Pallas kernels: none -> 1.73 us  [local(): pl.pallas_call(deliver, out_shape=shapes, in_specs=[vmem] * 4, out_specs=...]
    broadcast_in_dim x3 -> x0, local copies, waits for them, and re-layouts: 1.51 us -> none  [the longest x2 1.5 us: local(): jnp.broadcast_to(peak_offsets.reshape(2 * REACH, tiles, 1), (2 * REACH, t...]
    unnamed x2 -> x16, local copies, waits for them, and re-layouts: 5.44 us -> 6.92 us
    reshape x2 -> x0, local copies, waits for them, and re-layouts: 1.34 us -> none  [the longest x1 1.33 us: local(): targets[:2 * REACH, :tiles].reshape(1, 2 * REACH, rows_dev, columns)]
    pad x2 -> x0, local copies, waits for them, and re-layouts: 1.26 us -> none  [the longest x1 0.66 us: local(): lines = jnp.pad(weights, ((0, 8 - REACH), (tiles, 128 - 2 * tiles)))]
    squeeze x1 -> x0, local copies, waits for them, and re-layouts: 1.17 us -> none  [local(): rms[0, :ITERS]]
where the time goes in v2:
time: 72.5 us; the launch traced here: 72.1 us
  Pallas kernels  64.5 us (89%)
  local copies, waits for them, and re-layouts  6.92 us (10%)
    pallas_call x1, Pallas kernels, local(): pl.pallas_call(functools.partial(kernel, nz, nx, rows_dev, columns), out_...  62.8 us
    unnamed x16, local copies, waits for them, and re-layouts  6.92 us
    pallas_call x1, Pallas kernels, local(): pl.pallas_call(deliver, out_shape=shapes, in_specs=[vmem] * 4, out_specs=...  1.73 us

profile of v2, /device:TPU:0, one launch (start us, length us, event | category | flops | bytes accessed | tf_op | source)
XLA Modules:
  0.0 72.1 jit_solution(364727538739337383)
XLA Ops:
  0.6 0.0 copy-start
  0.6 1.2 %copy-done = bf16[1,2,16,128,128]{4,3,2,1,0:T(8,128)(2,1)S(1)} copy-done((bf16[1,2,16,128,128]{4,3,2,1,0:T(8,128)(2,1)S(1)}, bf16[1,2,16,128,128]{4,3,2,1,0:T(8,128)(2,1)}, u32[]{:S(2)}) %copy-start) | copy-done | bytes 1048600
  1.9 0.0 copy-start.1
  1.9 0.9 %copy-done.1 = bf16[256,256]{1,0:T(8,128)(2,1)S(1)} copy-done((bf16[256,256]{1,0:T(8,128)(2,1)S(1)}, bf16[256,256]{1,0:T(8,128)(2,1)}, u32[]{:S(2)}) %copy-start.1) | copy-done | bytes 131096
  2.8 0.0 copy-start.2
  2.8 0.9 %copy-done.2 = bf16[256,256]{1,0:T(8,128)(2,1)S(1)} copy-done((bf16[256,256]{1,0:T(8,128)(2,1)S(1)}, bf16[256,256]{1,0:T(8,128)(2,1)}, u32[]{:S(2)}) %copy-start.2) | copy-done | bytes 131096
  3.7 0.0 copy-start.3
  3.7 0.8 %copy-done.3 = f32[2,1,32,256]{3,2,1,0:T(8,128)S(1)} copy-done((f32[2,1,32,256]{3,2,1,0:T(8,128)S(1)}, f32[2,1,32,256]{3,2,1,0:T(8,128)}, u32[]{:S(2)}) %copy-start.3) | copy-done | bytes 65560
  4.5 0.0 copy-start.4
  4.5 0.8 %copy-done.4 = bf16[128,256]{1,0:T(8,128)(2,1)S(1)} copy-done((bf16[128,256]{1,0:T(8,128)(2,1)S(1)}, bf16[128,256]{1,0:T(8,128)(2,1)}, u32[]{:S(2)}) %copy-start.4) | copy-done | bytes 65560
  5.3 0.0 copy-start.5
  5.3 0.8 %copy-done.5 = bf16[128,256]{1,0:T(8,128)(2,1)S(1)} copy-done((bf16[128,256]{1,0:T(8,128)(2,1)S(1)}, bf16[128,256]{1,0:T(8,128)(2,1)}, u32[]{:S(2)}) %copy-start.5) | copy-done | bytes 65560
  6.2 0.0 copy-start.6
  6.2 0.7 copy-done.6
  6.9 0.0 copy-start.7
  6.9 0.7 copy-done.7
  7.6 62.8 %align.1 = (bf16[3,32,128,128]{3,2,1,0:T(8,128)(2,1)S(1)}, f32[6,2,16]{2,1,0:T(2,128)S(1)}, f32[2,32,256]{2,1,0:T(8,128)S(1)}, f32[4]{0:T(128)S(1)}) custom-call(bf16[32,128,128]{2,1,0:T(8,128)(2,1)S(1)} %bitcast.9, s32[6,2,16]{2,1,0:T(2,128)S(1)} %bitcast.11, s32[3,2,16]{2,1,0:T(2,128)S(1)} %bitcast.12, f32[2,32,256]{2,1,0:T(8,128)S(1)} %bitcast.10, ...), custom_call_target="tpu_custom_call" | custom-call | tf_op jit(solution)/shard_map/align/pallas_call | solution.py:514
  70.3 1.7 %deliver.1 = (bf16[3,32,128,128]{3,2,1,0:T(8,128)(2,1)}, f32[6,2,16]{2,1,0:T(2,128)}, f32[2,32,256]{2,1,0:T(8,128)}, f32[4]{0:T(128)}) custom-call(bf16[3,32,128,128]{3,2,1,0:T(8,128)(2,1)S(1)} %get-tuple-element.12.refs_0_, f32[6,2,16]{2,1,0:T(2,128)S(1)} %get-tuple-element.13.refs_1_, f32[2,32,256]{2,1,0:T(8,128)S(1)} %get-tuple-element.14.refs_2_, ...), custom_call_target="tpu_custom_call" | custom-call | tf_op jit(solution)/shard_map/deliver/pallas_call | solution.py:553
Async XLA Ops:
  0.6 1.2 %copy-start = (bf16[1,2,16,128,128]{4,3,2,1,0:T(8,128)(2,1)S(1)}, bf16[1,2,16,128,128]{4,3,2,1,0:T(8,128)(2,1)}, u32[]{:S(2)}) copy-start(bf16[1,2,16,128,128]{4,3,2,1,0:T(8,128)(2,1)} %param.8) | copy-start | bytes 3145732
  1.9 0.9 %copy-start.1 = (bf16[256,256]{1,0:T(8,128)(2,1)S(1)}, bf16[256,256]{1,0:T(8,128)(2,1)}, u32[]{:S(2)}) copy-start(bf16[256,256]{1,0:T(8,128)(2,1)} %constant.10.clone.t_back) | copy-start | bytes 393220
  2.8 0.9 %copy-start.2 = (bf16[256,256]{1,0:T(8,128)(2,1)S(1)}, bf16[256,256]{1,0:T(8,128)(2,1)}, u32[]{:S(2)}) copy-start(bf16[256,256]{1,0:T(8,128)(2,1)} %constant.9.clone.t_forward) | copy-start | bytes 393220
  3.7 0.8 %copy-start.3 = (f32[2,1,32,256]{3,2,1,0:T(8,128)S(1)}, f32[2,1,32,256]{3,2,1,0:T(8,128)}, u32[]{:S(2)}) copy-start(f32[2,1,32,256]{3,2,1,0:T(8,128)} %param.11) | copy-start | bytes 196612
  4.5 0.8 %copy-start.4 = (bf16[128,256]{1,0:T(8,128)(2,1)S(1)}, bf16[128,256]{1,0:T(8,128)(2,1)}, u32[]{:S(2)}) copy-start(bf16[128,256]{1,0:T(8,128)(2,1)} %constant.11.clone.t_last) | copy-start | bytes 196612
  5.3 0.8 %copy-start.5 = (bf16[128,256]{1,0:T(8,128)(2,1)S(1)}, bf16[128,256]{1,0:T(8,128)(2,1)}, u32[]{:S(2)}) copy-start(bf16[128,256]{1,0:T(8,128)(2,1)} %constant.8.clone.t_rows) | copy-start | bytes 196612
  6.2 0.7 copy-start.6
  6.9 0.7 copy-start.7
